TPU v7x, 32 devices: a whole 2x2x4 slice. The times are simulated.
32 devices in a mesh: groups: 2 (over x), ep: 16 (over z, y, core).
Axes of the slice: x: 2, y: 2, z: 4, core: 2. Of those that a mesh axis runs over, the one named last changes fastest.
Arguments:
- tokens: bfloat16 [4096, 3584], P(('groups', 'ep')), parts along dimension 0, may hold values from -6 to 6
- host: int32 [4096, 2], P(('groups', 'ep')), parts along dimension 0, may hold values from 0 to 7, all different within a row; in each aligned block of 128 rows (0 to 127, 128 to 255, ...) at most 40 rows name the same one
- copy: int32 [4096, 2], P(('groups', 'ep')), parts along dimension 0, may hold values from 0 to 1
- gate_prob: float32 [4096, 2], P(('groups', 'ep')), parts along dimension 0, may hold values from 0.1 to 1
- hot: int32 [8], replicated, may hold values from 0 to 7, each once
- w_gate: bfloat16 [16, 1792, 1024], P('ep'), may hold values from -0.09375 to 0.09375
- w_up: bfloat16 [16, 1792, 1024], P('ep'), may hold values from -0.09375 to 0.09375
- w_down: bfloat16 [16, 1024, 1792], P('ep'), may hold values from -0.1875 to 0.1875
- gate_scale: float32 [16, 14, 8], P('ep'), may hold values from 0.3 to 3
- up_scale: float32 [16, 14, 8], P('ep'), may hold values from 0.3 to 3
- down_scale: float32 [16, 8, 14], P('ep'), may hold values from 0.3 to 3
Outputs:
- mixed: bfloat16 [4096, 3584], P(('groups', 'ep')), parts along dimension 0
There are 2 independent parts, one for each index of `groups`. A program takes and returns all parts, laid end to end along the dimension named above; an argument that names none is the same for every part. Nothing has to cross between parts.
Inputs may be any that keep to these rules, and one draw needn't show every extreme that they name: Each row names 2 different host groups; no group is named by more than 40 of the rows of one device. `hot`: A permutation of the 8 experts.
All inputs are finite; a program needn't handle non-finite values.
Results may differ from a plain program's by a relative error of at most 0.0087.
Values may be sent and summed in bfloat16 or wider, within the bound.
A program may use at most 192 MiB of HBM per device.

v0:
```python
import functools

import jax
import jax.numpy as jnp
from jax import lax
from jax.experimental import pallas as pl
from jax.experimental.pallas import tpu as pltpu
from jax.sharding import PartitionSpec as P

SPLIT = 2


def from_partner(value, axis, apart):
    mask = 2**apart
    pairs = [(source, source ^ mask) for source in range(lax.axis_size(axis))]
    return lax.ppermute(value, axis, pairs)


def dequant(weight, scales):
    rows_in, cols_in = weight.shape
    row_blocks, col_blocks = scales.shape
    expanded = jnp.repeat(scales, cols_in // col_blocks, axis=1)
    blocks = (
        weight.reshape(row_blocks, rows_in // row_blocks, cols_in).astype(jnp.float32)
        * expanded[:, None, :]
    )
    return blocks.reshape(rows_in, cols_in).astype(jnp.bfloat16)


def lookup(table_in, keys):
    positions = jnp.arange(table_in.shape[0], dtype=jnp.int32)
    return jnp.sum(jnp.where(keys[:, None] == positions[None, :], table_in[None, :], 0), axis=1)


def padded_exchange(
    tokens, host, copy, gate_prob, hot, w_gate, w_up, w_down, gate_scale, up_scale, down_scale
):
    devices = lax.axis_size("ep")
    experts = devices // SPLIT
    tok_rows, width = tokens.shape
    top_count = host.shape[1]
    capacity = tok_rows * top_count * 5 // (4 * experts)
    half_width = width // SPLIT
    pair_count = tok_rows * top_count
    host_f = host.reshape(pair_count)
    copy_f = copy.reshape(pair_count)
    onehot = (host_f[:, None] == jnp.arange(experts, dtype=jnp.int32)[None, :]).astype(jnp.int32)
    slot_f = jnp.sum((jnp.cumsum(onehot, axis=0) - 1) * onehot, axis=1)
    expert_f = jnp.where(copy_f == 0, host_f, lookup(hot, host_f))
    place_f = copy_f * capacity + slot_f
    tok_split = tokens.reshape(tok_rows, SPLIT, half_width)
    own_gate = dequant(w_gate[0], gate_scale[0])
    own_up = dequant(w_up[0], up_scale[0])
    own_down = dequant(w_down[0], down_scale[0])
    zone_rows = 2 * capacity
    slots_all = experts * zone_rows
    slot_table = (
        jnp.zeros((slots_all,), jnp.int32)
        .at[expert_f * zone_rows + place_f]
        .set(jnp.arange(pair_count, dtype=jnp.int32) + 1)
    )
    slot_table = slot_table.reshape(experts, zone_rows)
    filled = slot_table > 0
    row_of = jnp.maximum(slot_table - 1, 0) // top_count
    picked = tok_split[row_of[:, None, :], jnp.arange(SPLIT, dtype=jnp.int32)[None, :, None]]
    picked = jnp.where(filled[:, None, :, None], picked, jnp.zeros_like(picked))
    outgoing_rows = picked.reshape(devices, zone_rows, half_width)
    received = lax.all_to_all(outgoing_rows, "ep", split_axis=0, concat_axis=0, tiled=True)

    def project(matrix_in, own_mat):
        return jnp.dot(matrix_in, own_mat, preferred_element_type=jnp.float32)

    gate_part = project(received, own_gate).astype(jnp.bfloat16)
    up_part = project(received, own_up).astype(jnp.bfloat16)
    partner_gate, partner_up = from_partner((gate_part, up_part), "ep", 0)
    gate_sum = gate_part.astype(jnp.float32) + partner_gate.astype(jnp.float32)
    up_sum = up_part.astype(jnp.float32) + partner_up.astype(jnp.float32)
    hidden = (jax.nn.silu(gate_sum) * up_sum).astype(jnp.bfloat16)
    results = project(hidden, own_down).astype(jnp.bfloat16)
    returned = lax.all_to_all(results, "ep", split_axis=0, concat_axis=0, tiled=True)
    back_four = returned.reshape(experts, SPLIT, zone_rows, half_width)
    values = back_four[
        expert_f[:, None], jnp.arange(SPLIT, dtype=jnp.int32)[None, :], place_f[:, None]
    ]
    values = values.reshape(tok_rows, top_count, width).astype(jnp.float32)
    mixed = jnp.sum(values * gate_prob[:, :, None], axis=1)
    return mixed.astype(jnp.bfloat16)


def pooled_slots(chip_tokens, top_count, chips):
    mean = chip_tokens * top_count // chips
    return -(-(mean * 13 // 8) // 8) * 8


def offset_of(step, chips):
    return chips // 2 + ((step + 1) // 2) * (1 - 2 * (step % 2))


def fused_kernel(
    chips,
    cores,
    groups,
    slots,
    tokens,
    host,
    copied,
    gate_prob,
    hot,
    w_gate,
    w_up,
    w_down,
    gate_scale,
    up_scale,
    down_scale,
    out,
    flag_out,
    tok_all,
    info_rows,
    info_all,
    gate_mat,
    up_mat,
    down_mat,
    first_rank,
    second_rank,
    send_rows,
    recv_rows,
    part_out,
    part_in,
    hidden_out,
    returned,
    total,
    mixed,
    flag_send,
    flag_recv,
    flag_far,
    local_sem,
    weight_sem,
    pair_send,
    pair_recv,
    row_send,
    row_recv,
    part_send,
    part_recv,
    back_send,
    back_recv,
    flag_ssem,
    flag_rsem,
    far_ssem,
    far_rsem,
):
    rows = tokens.shape[0]
    half = tokens.shape[1] // cores
    hidden_size = gate_mat.shape[1]
    me = lax.axis_index("ep")
    group = lax.axis_index("groups")
    chip = me // cores
    core = me % cores
    other = 1 - core
    partner = {"ep": chip * cores + other}

    def to_chip(offset):
        return {"ep": lax.rem(chip + offset, chips) * cores + core}

    def from_chip(offset):
        return {"ep": lax.rem(chip + chips - offset, chips) * cores + core}

    weight_copies = [
        pltpu.make_async_copy(w_gate.at[0], gate_mat, weight_sem.at[0]),
        pltpu.make_async_copy(w_up.at[0], up_mat, weight_sem.at[1]),
        pltpu.make_async_copy(w_down.at[0], down_mat, weight_sem.at[2]),
    ]
    for copy in weight_copies:
        copy.start()
    my_rows = pl.ds(pl.multiple_of(core * rows, rows), rows)
    your_rows = pl.ds(pl.multiple_of(other * rows, rows), rows)
    my_cols = pl.ds(pl.multiple_of(core * half, 128), half)
    your_cols = pl.ds(pl.multiple_of(other * half, 128), half)
    own_tok = pltpu.make_async_copy(
        tokens.at[:, my_cols], tok_all.at[my_rows, :], local_sem.at[0]
    )
    own_tok.start()
    named = host[...]
    moved = jnp.zeros_like(named)
    for name in range(chips):
        moved = jnp.where(named == name, hot[name], moved)
    expert = jnp.where(copied[...] == 0, named, moved).astype(jnp.float32)
    top_count = named.shape[0]
    info_rows[core] = jnp.concatenate(
        [expert, gate_prob[...], jnp.zeros((8 - 2 * top_count, rows), jnp.float32)], axis=0
    )

    barrier = pltpu.get_barrier_semaphore()
    pl.semaphore_signal(
        barrier, inc=1, device_id=partner, device_id_type=pl.DeviceIdType.MESH
    )
    for far in range(1, groups):
        pl.semaphore_signal(
            barrier,
            inc=1,
            device_id={"groups": lax.rem(group + far, groups)},
            device_id_type=pl.DeviceIdType.MESH,
        )

    @pl.loop(1, chips)
    def _(offset):
        pl.semaphore_signal(
            barrier,
            inc=1,
            device_id=to_chip(offset),
            device_id_type=pl.DeviceIdType.MESH,
        )

    pl.semaphore_wait(barrier, chips + groups - 1)

    def remote(source, target, send, recv, device):
        return pltpu.make_async_remote_copy(
            src_ref=source,
            dst_ref=target,
            send_sem=send,
            recv_sem=recv,
            device_id=device,
            device_id_type=pl.DeviceIdType.MESH,
        )

    pair_info = remote(
        info_rows.at[core], info_rows.at[core], pair_send.at[0], pair_recv.at[0], partner
    )
    pair_tok = remote(
        tokens.at[:, your_cols],
        tok_all.at[my_rows, :],
        pair_send.at[1],
        pair_recv.at[1],
        partner,
    )
    pair_info.start()
    pair_tok.start()
    pair_info.wait()
    for part in range(cores):
        info_all[part * rows : (part + 1) * rows, :] = info_rows[part].T

    pooled = cores * rows
    lanes = lax.broadcasted_iota(jnp.int32, (pooled, 128), 1)
    expert_a = info_all[:, 0:1].astype(jnp.int32)
    expert_b = info_all[:, 1:2].astype(jnp.int32)
    match_a = expert_a == lanes
    match_b = expert_b == lanes
    hot_a = match_a.astype(jnp.float32)
    hot_b = match_b.astype(jnp.float32)
    below = (
        lax.broadcasted_iota(jnp.int32, (pooled, pooled), 1)
        < lax.broadcasted_iota(jnp.int32, (pooled, pooled), 0)
    ).astype(jnp.float32).astype(jnp.bfloat16)
    rank_a = jnp.dot(below, hot_a.astype(jnp.bfloat16), preferred_element_type=jnp.float32)
    rank_b = jnp.dot(below, hot_b.astype(jnp.bfloat16), preferred_element_type=jnp.float32)
    count_a = jnp.sum(hot_a, axis=0, keepdims=True)
    count_b = jnp.sum(hot_b, axis=0, keepdims=True)
    first_rank[...] = jnp.where(match_a, rank_a, -1.0)
    second_rank[...] = jnp.where(match_b, rank_b + count_a, -1.0)
    most = jnp.max(count_a + count_b, axis=1, keepdims=True)
    flag_send[...] = jnp.broadcast_to((most > slots).astype(jnp.float32), flag_send.shape)

    def slot_columns(expert):
        mine = lanes == expert
        column_a = jnp.sum(jnp.where(mine, first_rank[...] + 1.0, 0.0), axis=1, keepdims=True)
        column_b = jnp.sum(jnp.where(mine, second_rank[...] + 1.0, 0.0), axis=1, keepdims=True)
        positions = lax.broadcasted_iota(jnp.int32, (pooled, slots), 1).astype(jnp.float32) + 1.0
        return column_a == positions, column_b == positions

    own_tok.wait()
    pair_tok.wait()

    def pick(offset):
        in_a, in_b = slot_columns(lax.rem(chip + offset, chips))
        chosen = (in_a | in_b).astype(jnp.float32).astype(jnp.bfloat16)
        return lax.dot_general(
            chosen,
            tok_all[...],
            (((0,), (0,)), ((), ())),
            preferred_element_type=jnp.float32,
        ).astype(jnp.bfloat16)

    @pl.loop(0, chips - 1)
    def _(step):
        offset = offset_of(step, chips)
        send_rows[offset] = pick(offset)
        remote(
            send_rows.at[offset],
            recv_rows.at[offset],
            row_send.at[offset],
            row_recv.at[offset],
            to_chip(offset),
        ).start()
        remote(
            flag_send,
            flag_recv.at[offset],
            flag_ssem.at[offset],
            flag_rsem.at[offset],
            to_chip(offset),
        ).start()

    recv_rows[0] = pick(0)

    block = gate_mat.shape[0] // gate_scale.shape[1]

    def dequant_in_place(copy, mat, scale_at):
        copy.wait()

        @pl.loop(0, mat.shape[0] // block)
        def _(piece):
            at = pl.ds(pl.multiple_of(piece * block, block), block)
            for column in range(mat.shape[1] // block):
                lanes_at = slice(column * block, (column + 1) * block)
                mat[at, lanes_at] = (
                    mat[at, lanes_at].astype(jnp.float32) * scale_at(piece, column)
                ).astype(jnp.bfloat16)

    dequant_in_place(weight_copies[0], gate_mat, lambda row, column: gate_scale[column, row])
    dequant_in_place(weight_copies[1], up_mat, lambda row, column: up_scale[column, row])
    dequant_in_place(weight_copies[2], down_mat, lambda row, column: down_scale[row, column])

    def first_half(offset):
        features = recv_rows[offset]
        part_out[offset, :, 0:hidden_size] = jnp.dot(
            features, gate_mat[...], preferred_element_type=jnp.float32
        ).astype(jnp.bfloat16)
        part_out[offset, :, hidden_size:] = jnp.dot(
            features, up_mat[...], preferred_element_type=jnp.float32
        ).astype(jnp.bfloat16)
        part_copy(offset).start()

    def part_copy(offset):
        return remote(
            part_out.at[offset],
            part_in.at[offset],
            part_send.at[offset],
            part_recv.at[offset],
            partner,
        )

    def second_half(offset):
        part_copy(offset).wait()
        gate = part_out[offset, :, 0:hidden_size].astype(jnp.float32) + part_in[
            offset, :, 0:hidden_size
        ].astype(jnp.float32)
        up = part_out[offset, :, hidden_size:].astype(jnp.float32) + part_in[
            offset, :, hidden_size:
        ].astype(jnp.float32)
        hidden = (gate * (1.0 / (1.0 + jnp.exp(-gate))) * up).astype(jnp.bfloat16)
        return jnp.dot(hidden, down_mat[...], preferred_element_type=jnp.float32).astype(
            jnp.bfloat16
        )

    def row_copy(offset):
        return remote(
            send_rows.at[offset],
            recv_rows.at[offset],
            row_send.at[offset],
            row_recv.at[offset],
            to_chip(offset),
        )

    def back_copy(offset):
        return remote(
            hidden_out.at[offset],
            returned.at[offset],
            back_send.at[offset],
            back_recv.at[offset],
            from_chip(offset),
        )

    first_half(0)

    @pl.loop(0, chips - 1)
    def _(step):
        offset = offset_of(step, chips)
        row_copy(offset).wait()
        first_half(offset)
        before = jnp.where(step == 0, 0, offset_of(step - 1, chips))
        result = second_half(before)

        @pl.when(step == 0)
        def _():
            returned[0] = result

        @pl.when(step > 0)
        def _():
            hidden_out[before] = result
            back_copy(before).start()

    last = offset_of(chips - 2, chips)
    hidden_out[last] = second_half(last)
    back_copy(last).start()

    flag_recv[0] = flag_send[...]

    @pl.loop(1, chips)
    def _(offset):
        remote(
            flag_send,
            flag_recv.at[offset],
            flag_ssem.at[offset],
            flag_rsem.at[offset],
            to_chip(offset),
        ).wait()

    flag_far[0] = jnp.max(flag_recv[...], axis=0)
    far_copies = [
        remote(
            flag_far.at[0],
            flag_far.at[far],
            far_ssem.at[far],
            far_rsem.at[far],
            {"groups": lax.rem(group + far, groups)},
        )
        for far in range(1, groups)
    ]
    for copy in far_copies:
        copy.start()
    total[...] = jnp.zeros_like(total)

    def add_returned(offset):
        in_a, in_b = slot_columns(lax.rem(chip + offset, chips))
        weight = jnp.where(in_a, info_all[:, 2:3], 0.0) + jnp.where(
            in_b, info_all[:, 3:4], 0.0
        )
        high = weight.astype(jnp.bfloat16)
        low = (weight - high.astype(jnp.float32)).astype(jnp.bfloat16)
        values = returned[offset]
        total[...] += jnp.dot(high, values, preferred_element_type=jnp.float32) + jnp.dot(
            low, values, preferred_element_type=jnp.float32
        )

    add_returned(0)

    @pl.loop(0, chips - 1)
    def _(step):
        offset = offset_of(step, chips)
        back_copy(offset).wait()
        add_returned(offset)

    mixed[...] = total[...].astype(jnp.bfloat16)
    own_out = pltpu.make_async_copy(
        mixed.at[my_rows, :], out.at[:, my_cols], local_sem.at[2]
    )
    pair_out = remote(
        mixed.at[your_rows, :],
        out.at[:, my_cols],
        pair_send.at[2],
        pair_recv.at[2],
        partner,
    )
    own_out.start()
    pair_out.start()

    for copy in far_copies:
        copy.wait()
    flag_out[0] = jnp.max(flag_far[...]).astype(jnp.int32)
    own_out.wait()
    pair_out.wait()


def per_device(
    tokens, host, copy, gate_prob, hot, w_gate, w_up, w_down, gate_scale, up_scale, down_scale
):
    cores = SPLIT
    chips = lax.axis_size("ep") // cores
    groups = lax.axis_size("groups")
    tok_rows, width = tokens.shape
    half = width // cores
    hidden_size = w_gate.shape[2]
    pooled = cores * tok_rows
    slots = pooled_slots(pooled, host.shape[1], chips)
    any_space = pl.BlockSpec(memory_space=pl.ANY)
    vmem_space = pl.BlockSpec(memory_space=pltpu.VMEM)
    smem_space = pl.BlockSpec(memory_space=pltpu.SMEM)
    dma = pltpu.SemaphoreType.DMA
    out, flag = pl.pallas_call(
        functools.partial(fused_kernel, chips, cores, groups, slots),
        out_shape=(
            jax.ShapeDtypeStruct((tok_rows, width), jnp.bfloat16),
            jax.ShapeDtypeStruct((1,), jnp.int32),
        ),
        in_specs=[any_space] + [vmem_space] * 3 + [smem_space] + [any_space] * 3 + [smem_space] * 3,
        out_specs=(any_space, smem_space),
        scratch_shapes=[
            pltpu.VMEM((pooled, half), jnp.bfloat16),
            pltpu.VMEM((cores, 8, tok_rows), jnp.float32),
            pltpu.VMEM((pooled, 8), jnp.float32),
            pltpu.VMEM(w_gate.shape[1:], jnp.bfloat16),
            pltpu.VMEM(w_up.shape[1:], jnp.bfloat16),
            pltpu.VMEM(w_down.shape[1:], jnp.bfloat16),
            pltpu.VMEM((pooled, 128), jnp.float32),
            pltpu.VMEM((pooled, 128), jnp.float32),
            pltpu.VMEM((chips, slots, half), jnp.bfloat16),
            pltpu.VMEM((chips, slots, half), jnp.bfloat16),
            pltpu.VMEM((chips, slots, 2 * hidden_size), jnp.bfloat16),
            pltpu.VMEM((chips, slots, 2 * hidden_size), jnp.bfloat16),
            pltpu.VMEM((chips, slots, half), jnp.bfloat16),
            pltpu.VMEM((chips, slots, half), jnp.bfloat16),
            pltpu.VMEM((pooled, half), jnp.float32),
            pltpu.VMEM((pooled, half), jnp.bfloat16),
            pltpu.VMEM((8, 128), jnp.float32),
            pltpu.VMEM((chips, 8, 128), jnp.float32),
            pltpu.VMEM((groups, 8, 128), jnp.float32),
            dma((3,)),
            dma((3,)),
            dma((3,)),
            dma((3,)),
            dma((chips,)),
            dma((chips,)),
            dma((chips,)),
            dma((chips,)),
            dma((chips,)),
            dma((chips,)),
            dma((chips,)),
            dma((chips,)),
            dma((groups,)),
            dma((groups,)),
        ],
        compiler_params=pltpu.CompilerParams(
            collective_id=0, has_side_effects=True, vmem_limit_bytes=60 * 1024 * 1024
        ),
    )(
        tokens,
        host.T,
        copy.T,
        gate_prob.T,
        hot,
        w_gate,
        w_up,
        w_down,
        gate_scale[0].T,
        up_scale[0].T,
        down_scale[0],
    )
    return lax.cond(
        flag[0] > 0,
        lambda: padded_exchange(
            tokens,
            host,
            copy,
            gate_prob,
            hot,
            w_gate,
            w_up,
            w_down,
            gate_scale,
            up_scale,
            down_scale,
        ),
        lambda: out,
    )


def solution(mesh):
    return jax.shard_map(
        per_device,
        mesh=mesh,
        in_specs=(
            P(("groups", "ep"), None),
            P(("groups", "ep"), None),
            P(("groups", "ep"), None),
            P(("groups", "ep"), None),
            P(),
            P("ep", None, None),
            P("ep", None, None),
            P("ep", None, None),
            P("ep", None, None),
            P("ep", None, None),
            P("ep", None, None),
        ),
        out_specs=P(("groups", "ep"), None),
        check_vma=False,
    )
```

profile of v0, /device:TPU:15, one launch (start us, length us, event | category | flops | bytes accessed | tf_op | source)
XLA Modules:
  0.0 149.5 jit_solution(3227991437990485785)
XLA Ops:
  0.0 0.0 copy-start.1
  0.0 0.0 copy-start.3
  0.0 0.0 copy-start.4
  0.0 0.0 copy-start.5
  0.0 0.0 copy-start.6
  0.0 0.0 copy-start.7
  0.0 0.0 copy-start.8
  0.0 0.0 copy-start.9
  0.1 147.6 %shard_map.111 = (bf16[128,3584]{1,0:T(8,128)(2,1)S(1)}, s32[1]{0:T(128)}) custom-call(bf16[128,3584]{1,0:T(8,128)(2,1)} %tokens.1, s32[2,128]{1,0:T(2,128)} %bitcast.80, s32[2,128]{1,0:T(2,128)} %bitcast.81, f32[2,128]{1,0:T(2,128)} %bitcast.82, s32[8]{0:T(128)} %hot.1, bf16[1,1792,1024]{2,1,0:T(8,128)(2,1)} %w_gate.1, bf16[1,1792,1024]{2,1,0:T(8,128)(2,1)} %w_up.1, ...), custom_call_target="tpu_custom_call" | custom-call | tf_op jit(solution)/shard_map/pallas_call | solution.py:477
  148.3 0.0 copy-done.1
  148.3 0.0 copy-done.3
  148.3 0.0 copy-done.4
  148.3 0.0 copy-done.5
  148.3 0.0 copy-done.6
  148.4 0.0 copy-done.7
  148.4 0.0 copy-done.8
  148.4 0.0 copy-done.9
  148.4 0.2 conditional.1
  148.6 0.9 copy.38
Async XLA Ops:
  0.0 148.3 %copy-start.1 = (bf16[128,3584]{1,0:T(8,128)(2,1)S(1)}, bf16[128,3584]{1,0:T(8,128)(2,1)}, u32[]{:S(2)}) copy-start(bf16[128,3584]{1,0:T(8,128)(2,1)} %tokens.1) | copy-start | bytes 2752516
  0.0 148.3 %copy-start.3 = (f32[1,14,8]{1,2,0:T(8,128)S(1)}, f32[1,14,8]{1,2,0:T(8,128)}, u32[]{:S(2)}) copy-start(f32[1,14,8]{1,2,0:T(8,128)} %param.21) | copy-start | bytes 1348
  0.0 148.3 %copy-start.4 = (f32[1,14,8]{1,2,0:T(8,128)S(1)}, f32[1,14,8]{1,2,0:T(8,128)}, u32[]{:S(2)}) copy-start(f32[1,14,8]{1,2,0:T(8,128)} %param.22) | copy-start | bytes 1348
  0.0 148.3 %copy-start.5 = (f32[1,8,14]{2,1,0:T(8,128)S(1)}, f32[1,8,14]{2,1,0:T(8,128)}, u32[]{:S(2)}) copy-start(f32[1,8,14]{2,1,0:T(8,128)} %param.23) | copy-start | bytes 1348
  0.0 148.3 %copy-start.6 = (s32[128,2]{0,1:T(2,128)S(1)}, s32[128,2]{0,1:T(2,128)}, u32[]{:S(2)}) copy-start(s32[128,2]{0,1:T(2,128)} %param.14) | copy-start | bytes 3076
  0.0 148.3 %copy-start.7 = (s32[128,2]{0,1:T(2,128)S(1)}, s32[128,2]{0,1:T(2,128)}, u32[]{:S(2)}) copy-start(s32[128,2]{0,1:T(2,128)} %param.15) | copy-start | bytes 3076
  0.0 148.3 %copy-start.8 = (f32[128,2]{0,1:T(2,128)S(1)}, f32[128,2]{0,1:T(2,128)}, u32[]{:S(2)}) copy-start(f32[128,2]{0,1:T(2,128)} %param.16) | copy-start | bytes 3076
  0.0 148.3 %copy-start.9 = (s32[8]{0:T(128)S(1)}, s32[8]{0:T(128)}, u32[]{:S(2)}) copy-start(s32[8]{0:T(128)} %hot.1) | copy-start | bytes 100
where the time goes:
time: 150 us
  Pallas kernels  148 us (99%)
    pallas_call x1, Pallas kernels, per_device(): pl.pallas_call(functools.partial(fused_kernel, chips, cores, groups, slot...  148 us

commit v1 on v0

--- a/solution.py
+++ b/solution.py
@@ -459,22 +459,699 @@
     pair_out.wait()
 
 
-def per_device(
-    tokens, host, copy, gate_prob, hot, w_gate, w_up, w_down, gate_scale, up_scale, down_scale
+FAR_CHUNKS = 2
+COLUMN_PARTS = 2
+
+
+def two_level_kernel(
+    groups,
+    slots,
+    tokens,
+    host,
+    copied,
+    gate_prob,
+    hot,
+    w_gate,
+    w_up,
+    w_down,
+    gate_scale,
+    up_scale,
+    down_scale,
+    out,
+    flag_out,
+    tok_all,
+    far_tok,
+    info_rows,
+    pool_info,
+    pool_rank,
+    gate_mat,
+    up_mat,
+    down_mat,
+    send_rows,
+    recv_rows,
+    part_out,
+    part_in,
+    hidden_out,
+    returned,
+    sum_out,
+    sum_in,
+    total,
+    mixed,
+    flag_send,
+    flag_recv,
+    flag_far,
+    local_sem,
+    weight_sem,
+    pair_send,
+    pair_recv,
+    info_send,
+    info_recv,
+    far_send,
+    far_recv,
+    row_send,
+    row_recv,
+    part_send,
+    part_recv,
+    back_send,
+    back_recv,
+    sum_send,
+    sum_recv,
+    out_sem,
+    out_send,
+    out_recv,
+    flag_ssem,
+    flag_rsem,
+    far_ssem,
+    far_rsem,
 ):
     cores = SPLIT
     chips = lax.axis_size("ep") // cores
-    groups = lax.axis_size("groups")
-    tok_rows, width = tokens.shape
-    half = width // cores
-    hidden_size = w_gate.shape[2]
+    rows = tokens.shape[0]
+    half = tokens.shape[1] // cores
+    piece = half // COLUMN_PARTS
+    few = rows // FAR_CHUNKS
+    pooled = cores * rows
+    hidden_size = gate_mat.shape[1]
+    top_count = host.shape[0]
+    me = lax.axis_index("ep")
+    group = lax.axis_index("groups")
+    chip = me // cores
+    core = me % cores
+    other = 1 - core
+    column = chip % 2
+    level = chip // 2
+    side = level // 2
+    inner = (level == 1) | (level == 2)
+    outer_index = jnp.where(inner, 0, 1)
+    far_inner = (2 - side) * 2 + column
+    far_outer = 3 * (1 - side) * 2 + column
+    partner = {"ep": chip * cores + other}
+
+    def at_chip(which, which_core=None):
+        return {"ep": which * cores + (core if which_core is None else which_core)}
+
+    def remote(source, target, send, recv, device):
+        return pltpu.make_async_remote_copy(
+            src_ref=source,
+            dst_ref=target,
+            send_sem=send,
+            recv_sem=recv,
+            device_id=device,
+            device_id_type=pl.DeviceIdType.MESH,
+        )
+
+    weight_copies = [
+        pltpu.make_async_copy(w_gate.at[0], gate_mat, weight_sem.at[0]),
+        pltpu.make_async_copy(w_up.at[0], up_mat, weight_sem.at[1]),
+        pltpu.make_async_copy(w_down.at[0], down_mat, weight_sem.at[2]),
+    ]
+    my_rows = pl.ds(pl.multiple_of(core * rows, rows), rows)
+    my_cols = pl.ds(pl.multiple_of(core * half, 128), half)
+    your_cols = pl.ds(pl.multiple_of(other * half, 128), half)
+    own_tok = pltpu.make_async_copy(
+        tokens.at[:, my_cols], tok_all.at[my_rows, :], local_sem.at[0]
+    )
+
+    barrier = pltpu.get_barrier_semaphore()
+    devices = cores * chips
+    for far in range(1, groups):
+        pl.semaphore_signal(
+            barrier,
+            inc=1,
+            device_id={"groups": lax.rem(group + far, groups)},
+            device_id_type=pl.DeviceIdType.MESH,
+        )
+
+    @pl.loop(1, devices)
+    def _(step):
+        pl.semaphore_signal(
+            barrier,
+            inc=1,
+            device_id={"ep": lax.rem(me + step, devices)},
+            device_id_type=pl.DeviceIdType.MESH,
+        )
+
+    own_tok.start()
+    for copy in weight_copies:
+        copy.start()
+    named = host[...]
+    moved = jnp.zeros_like(named)
+    for name in range(chips):
+        moved = jnp.where(named == name, hot[name], moved)
+    expert = jnp.where(copied[...] == 0, named, moved).astype(jnp.float32)
+    info_rows[core] = jnp.concatenate(
+        [expert, gate_prob[...], jnp.zeros((8 - 2 * top_count, rows), jnp.float32)], axis=0
+    )
+    pl.semaphore_wait(barrier, devices + groups - 2)
+
+    def far_copy(chunk, part, target):
+        return remote(
+            tokens.at[
+                pl.ds(pl.multiple_of(chunk * few, few), few),
+                pl.ds(pl.multiple_of(target * half + part * piece, 128), piece),
+            ],
+            far_tok.at[
+                chunk,
+                pl.ds(pl.multiple_of((outer_index * cores + core) * few, few), few),
+                pl.ds(pl.multiple_of(part * piece, 128), piece),
+            ],
+            far_send.at[(chunk * COLUMN_PARTS + part) * cores + target],
+            far_recv.at[(chunk * COLUMN_PARTS + part) * 2 * cores + outer_index * cores + core],
+            at_chip(far_inner, target),
+        )
+
+    def far_arrival(chunk, part, source):
+        return remote(
+            tokens.at[pl.ds(0, few), pl.ds(0, piece)],
+            far_tok.at[
+                chunk,
+                pl.ds(pl.multiple_of(source * few, few), few),
+                pl.ds(pl.multiple_of(part * piece, 128), piece),
+            ],
+            far_send.at[0],
+            far_recv.at[(chunk * COLUMN_PARTS + part) * 2 * cores + source],
+            partner,
+        )
+
+    def far_info(target):
+        return remote(
+            info_rows.at[core],
+            info_rows.at[cores + outer_index * cores + core],
+            info_send.at[target],
+            info_recv.at[outer_index * cores + core],
+            at_chip(far_inner, target),
+        )
+
+    pair_info = remote(
+        info_rows.at[core], info_rows.at[core], pair_send.at[0], pair_recv.at[0], partner
+    )
+    pair_tok = remote(
+        tokens.at[:, your_cols],
+        tok_all.at[my_rows, :],
+        pair_send.at[1],
+        pair_recv.at[1],
+        partner,
+    )
+    pair_info.start()
+    for target in range(cores):
+        far_info(target).start()
+    pair_tok.start()
+
+    @pl.loop(0, FAR_CHUNKS * COLUMN_PARTS)
+    def _(step):
+        for target in range(cores):
+            far_copy(step // COLUMN_PARTS, step % COLUMN_PARTS, target).start()
+
+    expert_ids = lax.broadcasted_iota(jnp.int32, (chips, pooled), 0)
+    near = (expert_ids // 4 == side).astype(jnp.float32)
+    before = (
+        lax.broadcasted_iota(jnp.int32, (pooled, pooled), 0)
+        < lax.broadcasted_iota(jnp.int32, (pooled, pooled), 1)
+    ).astype(jnp.float32).astype(jnp.bfloat16)
+
+    def rank_pool(pool, info):
+        pool_info[pool] = info
+        names = expert_ids.astype(jnp.float32)
+        hot_a = (info[0:1, :] == names).astype(jnp.float32)
+        hot_b = (info[1:2, :] == names).astype(jnp.float32)
+        both = jnp.concatenate([hot_a, hot_b], axis=0).astype(jnp.bfloat16)
+        ranks = jnp.dot(both, before, preferred_element_type=jnp.float32)
+        count_a = jnp.sum(hot_a, axis=1, keepdims=True)
+        count_b = jnp.sum(hot_b, axis=1, keepdims=True)
+        pool_rank[pool, 0:chips, :] = hot_a * (ranks[0:chips] + 1.0)
+        pool_rank[pool, chips:, :] = hot_b * (ranks[chips:] + count_a + 1.0)
+        counts = (count_a + count_b) * near
+        return jnp.max(jnp.max(counts, axis=1, keepdims=True), axis=0, keepdims=True)
+
+    def flag_of(most):
+        return jnp.broadcast_to((most > slots).astype(jnp.float32), flag_send.shape)
+
+    positions = lax.broadcasted_iota(jnp.int32, (slots, pooled), 0).astype(jnp.float32) + 1.0
+
+    def slot_rows(pool, mask):
+        mine = expert_ids == (chip ^ mask)
+        row_a = jnp.sum(
+            jnp.where(mine, pool_rank[pool, 0:chips, :], 0.0), axis=0, keepdims=True
+        )
+        row_b = jnp.sum(jnp.where(mine, pool_rank[pool, chips:, :], 0.0), axis=0, keepdims=True)
+        return row_a == positions, row_b == positions
+
+    def chosen_rows(pool, mask):
+        in_a, in_b = slot_rows(pool, mask)
+        return (in_a | in_b).astype(jnp.float32).astype(jnp.bfloat16)
+
+    def own_row_copy(mask):
+        return remote(
+            send_rows.at[mask],
+            recv_rows.at[mask],
+            row_send.at[mask * COLUMN_PARTS],
+            row_recv.at[mask * COLUMN_PARTS],
+            at_chip(chip ^ mask),
+        )
+
+    pair_info.wait()
+    own_most = rank_pool(0, jnp.concatenate([info_rows[0], info_rows[1]], axis=1))
+    flag_send[...] = flag_of(own_most)
+    own_tok.wait()
+    pair_tok.wait()
+
+    def pick_own(mask):
+        return jnp.dot(
+            chosen_rows(0, mask), tok_all[...], preferred_element_type=jnp.float32
+        ).astype(jnp.bfloat16)
+
+    @pl.loop(0, 3)
+    def _(step):
+        mask = lax.rem(step + 1, 3) + 1
+        send_rows[mask] = pick_own(mask)
+        own_row_copy(mask).start()
+
+    recv_rows[0] = pick_own(0)
+
+    @pl.when(inner)
+    def _():
+        for source in range(2 * cores):
+            remote(
+                info_rows.at[0],
+                info_rows.at[cores + source],
+                info_send.at[0],
+                info_recv.at[source],
+                partner,
+            ).wait_recv()
+        left = lax.broadcasted_iota(jnp.int32, (8, rows), 1) < few
+        turned = [pltpu.roll(info_rows[cores + source], few, 1) for source in range(2 * cores)]
+        first = [
+            jnp.where(left, info_rows[cores + 2 * pair], turned[2 * pair + 1])
+            for pair in range(cores)
+        ]
+        second = [
+            jnp.where(left, turned[2 * pair], info_rows[cores + 2 * pair + 1])
+            for pair in range(cores)
+        ]
+        most_a = rank_pool(1, jnp.concatenate(first, axis=1))
+        most_b = rank_pool(2, jnp.concatenate(second, axis=1))
+        flag_send[...] = flag_of(jnp.maximum(own_most, jnp.maximum(most_a, most_b)))
+
+    def flag_copy(offset):
+        return remote(
+            flag_send,
+            flag_recv.at[offset],
+            flag_ssem.at[offset],
+            flag_rsem.at[offset],
+            at_chip(lax.rem(chip + offset, chips)),
+        )
+
+    @pl.loop(1, chips)
+    def _(offset):
+        flag_copy(offset).start()
+
+    block = gate_mat.shape[0] // gate_scale.shape[1]
+
+    def dequant_in_place(copy, mat, scale_at):
+        copy.wait()
+
+        @pl.loop(0, mat.shape[0] // block)
+        def _(strip):
+            at = pl.ds(pl.multiple_of(strip * block, block), block)
+            for lane_block in range(mat.shape[1] // block):
+                lanes_at = slice(lane_block * block, (lane_block + 1) * block)
+                mat[at, lanes_at] = (
+                    mat[at, lanes_at].astype(jnp.float32) * scale_at(strip, lane_block)
+                ).astype(jnp.bfloat16)
+
+    dequant_in_place(weight_copies[0], gate_mat, lambda row, lane: gate_scale[lane, row])
+    dequant_in_place(weight_copies[1], up_mat, lambda row, lane: up_scale[lane, row])
+    dequant_in_place(weight_copies[2], down_mat, lambda row, lane: down_scale[row, lane])
+
+    def part_cols(part):
+        return pl.ds(pl.multiple_of(part * piece, 128), piece)
+
+    def relay_copy(chunk, mask, part):
+        target_group = 4 + 2 * chunk + mask % 2
+        return remote(
+            send_rows.at[4 + 4 * chunk + mask, :, part_cols(part)],
+            recv_rows.at[target_group, :, part_cols(part)],
+            row_send.at[(4 + 4 * chunk + mask) * COLUMN_PARTS + part],
+            row_recv.at[target_group * COLUMN_PARTS + part],
+            at_chip(chip ^ mask),
+        )
+
+    def relay(chunk):
+        @pl.loop(0, COLUMN_PARTS)
+        def _(part):
+            for source in range(2 * cores):
+                far_arrival(chunk, part, source).wait_recv()
+
+            @pl.loop(0, 4)
+            def _(step):
+                mask = jnp.where(step < 2, step + 2, 3 - step)
+                picked = jnp.dot(
+                    chosen_rows(1 + chunk, mask),
+                    far_tok[chunk, :, part_cols(part)],
+                    preferred_element_type=jnp.float32,
+                ).astype(jnp.bfloat16)
+
+                @pl.when(mask == 0)
+                def _():
+                    recv_rows[4 + 2 * chunk, :, part_cols(part)] = picked
+
+                @pl.when(mask != 0)
+                def _():
+                    send_rows[4 + 4 * chunk + mask, :, part_cols(part)] = picked
+                    relay_copy(chunk, mask, part).start()
+
+    def wait_rows(slot_group):
+        @pl.when((slot_group > 0) & (slot_group < 4))
+        def _():
+            own_row_copy(slot_group).wait_recv()
+
+        @pl.when((slot_group >= 4) & ~(inner & (slot_group % 2 == 0)))
+        def _():
+            for part in range(COLUMN_PARTS):
+                remote(
+                    send_rows.at[0, :, part_cols(part)],
+                    recv_rows.at[slot_group, :, part_cols(part)],
+                    row_send.at[0],
+                    row_recv.at[slot_group * COLUMN_PARTS + part],
+                    partner,
+                ).wait_recv()
+
+    def part_copy(slot_group):
+        return remote(
+            part_out.at[slot_group],
+            part_in.at[slot_group],
+            part_send.at[slot_group],
+            part_recv.at[slot_group],
+            partner,
+        )
+
+    def first_half(slot_group):
+        wait_rows(slot_group)
+        features = recv_rows[slot_group]
+        part_out[slot_group, :, 0:hidden_size] = jnp.dot(
+            features, gate_mat[...], preferred_element_type=jnp.float32
+        ).astype(jnp.bfloat16)
+        part_out[slot_group, :, hidden_size:] = jnp.dot(
+            features, up_mat[...], preferred_element_type=jnp.float32
+        ).astype(jnp.bfloat16)
+        part_copy(slot_group).start()
+
+    def home_of(slot_group):
+        own = slot_group < 4
+        mask = jnp.where(own, slot_group, slot_group % 2 + jnp.where(inner, 0, 2))
+        pool = jnp.where(own, 0, slot_group // 2 - 1)
+        return pool, mask
+
+    def back_copy(slot_group, part):
+        pool, mask = home_of(slot_group)
+        return remote(
+            hidden_out.at[slot_group, :, part_cols(part)],
+            returned.at[pool * 4 + mask, :, part_cols(part)],
+            back_send.at[slot_group * COLUMN_PARTS + part],
+            back_recv.at[(pool * 4 + mask) * COLUMN_PARTS + part],
+            at_chip(chip ^ mask),
+        )
+
+    def second_half(slot_group):
+        part_copy(slot_group).wait()
+        gate = part_out[slot_group, :, 0:hidden_size].astype(jnp.float32) + part_in[
+            slot_group, :, 0:hidden_size
+        ].astype(jnp.float32)
+        up = part_out[slot_group, :, hidden_size:].astype(jnp.float32) + part_in[
+            slot_group, :, hidden_size:
+        ].astype(jnp.float32)
+        hidden = (gate * (1.0 / (1.0 + jnp.exp(-gate))) * up).astype(jnp.bfloat16)
+        pool, mask = home_of(slot_group)
+        for part in range(COLUMN_PARTS):
+            cols = slice(part * piece, (part + 1) * piece)
+            result = jnp.dot(
+                hidden, down_mat[:, cols], preferred_element_type=jnp.float32
+            ).astype(jnp.bfloat16)
+
+            @pl.when(mask == 0)
+            def _():
+                returned[pool * 4, :, cols] = result
+
+            @pl.when(mask != 0)
+            def _():
+                hidden_out[slot_group, :, cols] = result
+                back_copy(slot_group, part).start()
+
+    def back_arrival(pool, mask, part):
+        return remote(
+            hidden_out.at[0, :, part_cols(part)],
+            returned.at[pool * 4 + mask, :, part_cols(part)],
+            back_send.at[0],
+            back_recv.at[(pool * 4 + mask) * COLUMN_PARTS + part],
+            partner,
+        )
+
+    def combined(pool, part):
+        acc = None
+        for mask in range(4):
+            if mask:
+                back_arrival(pool, mask, part).wait_recv()
+            in_a, in_b = slot_rows(pool, mask)
+            weight = jnp.where(in_a, pool_info[pool, top_count : top_count + 1, :], 0.0)
+            weight += jnp.where(in_b, pool_info[pool, top_count + 1 : top_count + 2, :], 0.0)
+            high = weight.astype(jnp.bfloat16)
+            low = (weight - high.astype(jnp.float32)).astype(jnp.bfloat16)
+            values = returned[pool * 4 + mask, :, part_cols(part)]
+            for term in (high, low):
+                product = lax.dot_general(
+                    term, values, (((0,), (0,)), ((), ())), preferred_element_type=jnp.float32
+                )
+                acc = product if acc is None else acc + product
+        return acc
+
+    def sum_copy(chunk, part, which):
+        return remote(
+            sum_out.at[chunk, which * rows : (which + 1) * rows, part_cols(part)],
+            sum_in.at[chunk, :, part_cols(part)],
+            sum_send.at[(chunk * COLUMN_PARTS + part) * 2 + which],
+            sum_recv.at[chunk * COLUMN_PARTS + part],
+            at_chip(far_outer if which else far_inner),
+        )
+
+    def return_sums(chunk):
+        @pl.loop(0, COLUMN_PARTS)
+        def _(part):
+            sum_out[chunk, :, part_cols(part)] = combined(1 + chunk, part).astype(jnp.bfloat16)
+            for which in range(2):
+                sum_copy(chunk, part, which).start()
+
+    @pl.loop(0, 5)
+    def _(turn):
+        @pl.when(inner & (turn >= 1) & (turn <= FAR_CHUNKS))
+        def _():
+            relay(turn - 1)
+
+        @pl.when(inner & (turn >= 3))
+        def _():
+            return_sums(turn - 3)
+
+        @pl.when(turn < 4)
+        def _():
+            position = jnp.where(
+                inner & (turn >= 1), jnp.where(turn == 3, 1, turn + 1), turn
+            )
+
+            @pl.loop(0, 2)
+            def _(which):
+                first_half(2 * position + which)
+
+            @pl.loop(0, 2)
+            def _(which):
+                second_half(2 * position + which)
+
+    flag_recv[0] = flag_send[...]
+
+    @pl.loop(1, chips)
+    def _(offset):
+        flag_copy(offset).wait()
+
+    flag_far[0] = jnp.max(flag_recv[...], axis=0)
+    far_copies = [
+        remote(
+            flag_far.at[0],
+            flag_far.at[far],
+            far_ssem.at[far],
+            far_rsem.at[far],
+            {"groups": lax.rem(group + far, groups)},
+        )
+        for far in range(1, groups)
+    ]
+    for copy in far_copies:
+        copy.start()
+
+    @pl.loop(0, COLUMN_PARTS)
+    def _(part):
+        total[:, part_cols(part)] = combined(0, part)
+
+    def out_rows(owner, chunk):
+        return pl.ds(pl.multiple_of(owner * rows + chunk * few, few), few)
+
+    def out_cols(part):
+        return pl.ds(pl.multiple_of(core * half + part * piece, 128), piece)
+
+    def own_out(chunk, part):
+        return pltpu.make_async_copy(
+            mixed.at[out_rows(core, chunk), part_cols(part)],
+            out.at[chunk * few : (chunk + 1) * few, out_cols(part)],
+            out_sem.at[chunk * COLUMN_PARTS + part],
+        )
+
+    def pair_out(chunk, part):
+        return remote(
+            mixed.at[out_rows(other, chunk), part_cols(part)],
+            out.at[chunk * few : (chunk + 1) * few, out_cols(part)],
+            out_send.at[chunk * COLUMN_PARTS + part],
+            out_recv.at[chunk * COLUMN_PARTS + part],
+            partner,
+        )
+
+    for chunk in range(FAR_CHUNKS):
+        for part in range(COLUMN_PARTS):
+            cols = slice(part * piece, (part + 1) * piece)
+            remote(
+                sum_out.at[0, 0:rows, cols],
+                sum_in.at[chunk, :, cols],
+                sum_send.at[0],
+                sum_recv.at[chunk * COLUMN_PARTS + part],
+                partner,
+            ).wait_recv()
+            for owner in range(cores):
+                at = slice(owner * rows + chunk * few, owner * rows + (chunk + 1) * few)
+                mixed[at, cols] = (
+                    total[at, cols]
+                    + sum_in[chunk, owner * few : (owner + 1) * few, cols].astype(jnp.float32)
+                ).astype(jnp.bfloat16)
+            pair_out(chunk, part).start()
+            own_out(chunk, part).start()
+
+    for copy in far_copies:
+        copy.wait()
+    flag_out[0] = jnp.max(flag_far[...]).astype(jnp.int32)
+
+    for target in range(cores):
+        far_info(target).wait_send()
+
+    @pl.loop(0, FAR_CHUNKS * COLUMN_PARTS)
+    def _(step):
+        for target in range(cores):
+            far_copy(step // COLUMN_PARTS, step % COLUMN_PARTS, target).wait_send()
+
+    @pl.loop(1, 4)
+    def _(mask):
+        own_row_copy(mask).wait_send()
+
+    @pl.loop(0, 8)
+    def _(slot_group):
+        _, mask = home_of(slot_group)
+
+        @pl.when(mask != 0)
+        def _():
+            for part in range(COLUMN_PARTS):
+                back_copy(slot_group, part).wait_send()
+
+    @pl.when(inner)
+    def _():
+        @pl.loop(0, FAR_CHUNKS * COLUMN_PARTS)
+        def _(step):
+            chunk = step // COLUMN_PARTS
+            part = step % COLUMN_PARTS
+            for which in range(2):
+                sum_copy(chunk, part, which).wait_send()
+
+            @pl.loop(1, 4)
+            def _(mask):
+                relay_copy(chunk, mask, part).wait_send()
+
+    for chunk in range(FAR_CHUNKS):
+        for part in range(COLUMN_PARTS):
+            own_out(chunk, part).wait()
+            pair_out(chunk, part).wait()
+
+
+def two_level_call(slots, tok_rows, half, hidden_size, groups, weight_shapes):
+    cores = SPLIT
+    chips = lax.axis_size("ep") // cores
     pooled = cores * tok_rows
-    slots = pooled_slots(pooled, host.shape[1], chips)
+    dma = pltpu.SemaphoreType.DMA
+    pieces = FAR_CHUNKS * COLUMN_PARTS
+    any_space = pl.BlockSpec(memory_space=pl.ANY)
+    vmem_space = pl.BlockSpec(memory_space=pltpu.VMEM)
+    smem_space = pl.BlockSpec(memory_space=pltpu.SMEM)
+    bf16, f32 = jnp.bfloat16, jnp.float32
+    return pl.pallas_call(
+        functools.partial(two_level_kernel, groups, slots),
+        out_shape=(
+            jax.ShapeDtypeStruct((tok_rows, cores * half), bf16),
+            jax.ShapeDtypeStruct((1,), jnp.int32),
+        ),
+        in_specs=[any_space] + [vmem_space] * 3 + [smem_space] + [any_space] * 3 + [smem_space] * 3,
+        out_specs=(any_space, smem_space),
+        scratch_shapes=[
+            pltpu.VMEM((pooled, half), bf16),
+            pltpu.VMEM((FAR_CHUNKS, pooled, half), bf16),
+            pltpu.VMEM((3 * cores, 8, tok_rows), f32),
+            pltpu.VMEM((3, 8, pooled), f32),
+            pltpu.VMEM((3, 2 * chips, pooled), f32),
+            pltpu.VMEM(weight_shapes[0], bf16),
+            pltpu.VMEM(weight_shapes[1], bf16),
+            pltpu.VMEM(weight_shapes[2], bf16),
+            pltpu.VMEM((12, slots, half), bf16),
+            pltpu.VMEM((8, slots, half), bf16),
+            pltpu.VMEM((8, slots, 2 * hidden_size), bf16),
+            pltpu.VMEM((8, slots, 2 * hidden_size), bf16),
+            pltpu.VMEM((8, slots, half), bf16),
+            pltpu.VMEM((12, slots, half), bf16),
+            pltpu.VMEM((FAR_CHUNKS, pooled, half), bf16),
+            pltpu.VMEM((FAR_CHUNKS, tok_rows, half), bf16),
+            pltpu.VMEM((pooled, half), f32),
+            pltpu.VMEM((pooled, half), bf16),
+            pltpu.VMEM((8, 128), f32),
+            pltpu.VMEM((chips, 8, 128), f32),
+            pltpu.VMEM((groups, 8, 128), f32),
+            dma((1,)),
+            dma((3,)),
+            dma((2,)),
+            dma((2,)),
+            dma((cores,)),
+            dma((2 * cores,)),
+            dma((pieces * cores,)),
+            dma((pieces * 2 * cores,)),
+            dma((12 * COLUMN_PARTS,)),
+            dma((8 * COLUMN_PARTS,)),
+            dma((8,)),
+            dma((8,)),
+            dma((8 * COLUMN_PARTS,)),
+            dma((12 * COLUMN_PARTS,)),
+            dma((pieces * 2,)),
+            dma((pieces,)),
+            dma((pieces,)),
+            dma((pieces,)),
+            dma((pieces,)),
+            dma((chips,)),
+            dma((chips,)),
+            dma((groups,)),
+            dma((groups,)),
+        ],
+        compiler_params=pltpu.CompilerParams(
+            collective_id=0, has_side_effects=True, vmem_limit_bytes=62 * 1024 * 1024
+        ),
+    )
+
+
+def direct_call(chips, slots, tok_rows, half, hidden_size, groups, weight_shapes):
+    cores = SPLIT
+    width = cores * half
+    pooled = cores * tok_rows
     any_space = pl.BlockSpec(memory_space=pl.ANY)
     vmem_space = pl.BlockSpec(memory_space=pltpu.VMEM)
     smem_space = pl.BlockSpec(memory_space=pltpu.SMEM)
     dma = pltpu.SemaphoreType.DMA
-    out, flag = pl.pallas_call(
+    return pl.pallas_call(
         functools.partial(fused_kernel, chips, cores, groups, slots),
         out_shape=(
             jax.ShapeDtypeStruct((tok_rows, width), jnp.bfloat16),
@@ -486,9 +1163,9 @@
             pltpu.VMEM((pooled, half), jnp.bfloat16),
             pltpu.VMEM((cores, 8, tok_rows), jnp.float32),
             pltpu.VMEM((pooled, 8), jnp.float32),
-            pltpu.VMEM(w_gate.shape[1:], jnp.bfloat16),
-            pltpu.VMEM(w_up.shape[1:], jnp.bfloat16),
-            pltpu.VMEM(w_down.shape[1:], jnp.bfloat16),
+            pltpu.VMEM(weight_shapes[0], jnp.bfloat16),
+            pltpu.VMEM(weight_shapes[1], jnp.bfloat16),
+            pltpu.VMEM(weight_shapes[2], jnp.bfloat16),
             pltpu.VMEM((pooled, 128), jnp.float32),
             pltpu.VMEM((pooled, 128), jnp.float32),
             pltpu.VMEM((chips, slots, half), jnp.bfloat16),
@@ -520,7 +1197,25 @@
         compiler_params=pltpu.CompilerParams(
             collective_id=0, has_side_effects=True, vmem_limit_bytes=60 * 1024 * 1024
         ),
-    )(
+    )
+
+
+def two_level_fits(chips, tok_rows, half):
+    return chips == 8 and tok_rows == 128 and half % (128 * COLUMN_PARTS) == 0
+
+
+def per_device(
+    tokens, host, copy, gate_prob, hot, w_gate, w_up, w_down, gate_scale, up_scale, down_scale
+):
+    cores = SPLIT
+    chips = lax.axis_size("ep") // cores
+    groups = lax.axis_size("groups")
+    tok_rows, width = tokens.shape
+    half = width // cores
+    hidden_size = w_gate.shape[2]
+    pooled = cores * tok_rows
+    slots = pooled_slots(pooled, host.shape[1], chips)
+    args = (
         tokens,
         host.T,
         copy.T,
@@ -533,6 +1228,12 @@
         up_scale[0].T,
         down_scale[0],
     )
+    weight_shapes = (w_gate.shape[1:], w_up.shape[1:], w_down.shape[1:])
+    if two_level_fits(chips, tok_rows, half):
+        call = two_level_call(slots, tok_rows, half, hidden_size, groups, weight_shapes)
+    else:
+        call = direct_call(chips, slots, tok_rows, half, hidden_size, groups, weight_shapes)
+    out, flag = call(*args)
     return lax.cond(
         flag[0] > 0,
         lambda: padded_exchange(

time: 150 us -> 145 us (0.967)
  the two profiles are of different devices: /device:TPU:15 before, /device:TPU:0 now
where the time goes in v1:
time: 145 us
  Pallas kernels  142 us (98%)
  local copies, waits for them, and re-layouts  2.19 us (2%)
    pallas_call x1, Pallas kernels, per_device(): out, flag = call(*args)  142 us

profile of v1, /device:TPU:0, one launch (start us, length us, event | category | flops | bytes accessed | tf_op | source)
XLA Modules:
  0.0 144.9 jit_solution(7642644274759937224)
XLA Ops:
  0.0 0.0 copy-start.1
  0.0 0.0 copy-start.3
  0.0 0.0 copy-start.4
  0.0 0.0 copy-start.5
  0.0 0.0 copy-start.6
  0.0 0.0 copy-start.7
  0.0 0.0 copy-start.8
  0.0 0.0 copy-start.9
  0.0 141.7 %shard_map.111 = (bf16[128,3584]{1,0:T(8,128)(2,1)}, s32[1]{0:T(128)}) custom-call(bf16[128,3584]{1,0:T(8,128)(2,1)} %tokens.1, s32[2,128]{1,0:T(2,128)} %bitcast.80, s32[2,128]{1,0:T(2,128)} %bitcast.81, f32[2,128]{1,0:T(2,128)} %bitcast.82, s32[8]{0:T(128)} %hot.1, bf16[1,1792,1024]{2,1,0:T(8,128)(2,1)} %w_gate.1, bf16[1,1792,1024]{2,1,0:T(8,128)(2,1)} %w_up.1, ...), custom_call_target="tpu_custom_call" | custom-call | tf_op jit(solution)/shard_map/pallas_call | solution.py:1236
  142.4 0.0 copy-done.1
  142.4 0.0 copy-done.3
  142.4 0.0 copy-done.4
  142.4 0.0 copy-done.5
  142.4 0.0 copy-done.6
  142.5 0.0 copy-done.7
  142.5 0.0 copy-done.8
  142.5 0.0 copy-done.9
  142.5 0.2 conditional.1
  142.7 2.2 %copy.38 = bf16[128,3584]{1,0:T(8,128)(2,1)} copy(bf16[128,3584]{1,0:T(8,128)(2,1)} %get-tuple-element.46) | data formatting | bytes 1835008
Async XLA Ops:
  0.0 142.4 %copy-start.1 = (bf16[128,3584]{1,0:T(8,128)(2,1)S(1)}, bf16[128,3584]{1,0:T(8,128)(2,1)}, u32[]{:S(2)}) copy-start(bf16[128,3584]{1,0:T(8,128)(2,1)} %tokens.1) | copy-start | bytes 2752516
  0.0 142.4 %copy-start.3 = (f32[1,14,8]{1,2,0:T(8,128)S(1)}, f32[1,14,8]{1,2,0:T(8,128)}, u32[]{:S(2)}) copy-start(f32[1,14,8]{1,2,0:T(8,128)} %param.21) | copy-start | bytes 1348
  0.0 142.4 %copy-start.4 = (f32[1,14,8]{1,2,0:T(8,128)S(1)}, f32[1,14,8]{1,2,0:T(8,128)}, u32[]{:S(2)}) copy-start(f32[1,14,8]{1,2,0:T(8,128)} %param.22) | copy-start | bytes 1348
  0.0 142.4 %copy-start.5 = (f32[1,8,14]{2,1,0:T(8,128)S(1)}, f32[1,8,14]{2,1,0:T(8,128)}, u32[]{:S(2)}) copy-start(f32[1,8,14]{2,1,0:T(8,128)} %param.23) | copy-start | bytes 1348
  0.0 142.4 %copy-start.6 = (s32[128,2]{0,1:T(2,128)S(1)}, s32[128,2]{0,1:T(2,128)}, u32[]{:S(2)}) copy-start(s32[128,2]{0,1:T(2,128)} %param.14) | copy-start | bytes 3076
  0.0 142.4 %copy-start.7 = (s32[128,2]{0,1:T(2,128)S(1)}, s32[128,2]{0,1:T(2,128)}, u32[]{:S(2)}) copy-start(s32[128,2]{0,1:T(2,128)} %param.15) | copy-start | bytes 3076
  0.0 142.4 %copy-start.8 = (f32[128,2]{0,1:T(2,128)S(1)}, f32[128,2]{0,1:T(2,128)}, u32[]{:S(2)}) copy-start(f32[128,2]{0,1:T(2,128)} %param.16) | copy-start | bytes 3076
  0.0 142.4 %copy-start.9 = (s32[8]{0:T(128)S(1)}, s32[8]{0:T(128)}, u32[]{:S(2)}) copy-start(s32[8]{0:T(128)} %hot.1) | copy-start | bytes 100

commit v2 on v1

--- a/solution.py
+++ b/solution.py
@@ -460,6 +460,8 @@
 
 
 FAR_CHUNKS = 2
+INNER_TURNS = ((0,), (4, 1), (5,), (6, 2), (7,), (3,), (), ())
+OUTER_TURNS = ((0, 1), (2,), (4, 5), (3,), (6, 7), (), (), ())
 COLUMN_PARTS = 2
 
 
@@ -529,7 +531,6 @@
     rows = tokens.shape[0]
     half = tokens.shape[1] // cores
     piece = half // COLUMN_PARTS
-    few = rows // FAR_CHUNKS
     pooled = cores * rows
     hidden_size = gate_mat.shape[1]
     top_count = host.shape[0]
@@ -542,7 +543,7 @@
     level = chip // 2
     side = level // 2
     inner = (level == 1) | (level == 2)
-    outer_index = jnp.where(inner, 0, 1)
+    my_chunk = jnp.where(inner, 1, 0)
     far_inner = (2 - side) * 2 + column
     far_outer = 3 * (1 - side) * 2 + column
     partner = {"ep": chip * cores + other}
@@ -560,6 +561,9 @@
             device_id_type=pl.DeviceIdType.MESH,
         )
 
+    def part_cols(part):
+        return pl.ds(pl.multiple_of(part * piece, 128), piece)
+
     weight_copies = [
         pltpu.make_async_copy(w_gate.at[0], gate_mat, weight_sem.at[0]),
         pltpu.make_async_copy(w_up.at[0], up_mat, weight_sem.at[1]),
@@ -567,6 +571,7 @@
     ]
     my_rows = pl.ds(pl.multiple_of(core * rows, rows), rows)
     my_cols = pl.ds(pl.multiple_of(core * half, 128), half)
+    your_rows = pl.ds(pl.multiple_of(other * rows, rows), rows)
     your_cols = pl.ds(pl.multiple_of(other * half, 128), half)
     own_tok = pltpu.make_async_copy(
         tokens.at[:, my_cols], tok_all.at[my_rows, :], local_sem.at[0]
@@ -602,44 +607,43 @@
     info_rows[core] = jnp.concatenate(
         [expert, gate_prob[...], jnp.zeros((8 - 2 * top_count, rows), jnp.float32)], axis=0
     )
-    pl.semaphore_wait(barrier, devices + groups - 2)
-
-    def far_copy(chunk, part, target):
-        return remote(
-            tokens.at[
-                pl.ds(pl.multiple_of(chunk * few, few), few),
-                pl.ds(pl.multiple_of(target * half + part * piece, 128), piece),
-            ],
-            far_tok.at[
-                chunk,
-                pl.ds(pl.multiple_of((outer_index * cores + core) * few, few), few),
-                pl.ds(pl.multiple_of(part * piece, 128), piece),
-            ],
-            far_send.at[(chunk * COLUMN_PARTS + part) * cores + target],
-            far_recv.at[(chunk * COLUMN_PARTS + part) * 2 * cores + outer_index * cores + core],
+    with jax.named_scope("k_barrier"):
+        pl.semaphore_wait(barrier, devices + groups - 2)
+
+    def far_copy(part, target):
+        return remote(
+            tokens.at[:, pl.ds(pl.multiple_of(target * half + part * piece, 128), piece)],
+            far_tok.at[my_chunk, my_rows, part_cols(part)],
+            far_send.at[part * cores + target],
+            far_recv.at[(my_chunk * COLUMN_PARTS + part) * cores + core],
             at_chip(far_inner, target),
         )
 
     def far_arrival(chunk, part, source):
         return remote(
-            tokens.at[pl.ds(0, few), pl.ds(0, piece)],
-            far_tok.at[
-                chunk,
-                pl.ds(pl.multiple_of(source * few, few), few),
-                pl.ds(pl.multiple_of(part * piece, 128), piece),
-            ],
+            tokens.at[:, pl.ds(0, piece)],
+            far_tok.at[chunk, pl.ds(source * rows, rows), part_cols(part)],
             far_send.at[0],
-            far_recv.at[(chunk * COLUMN_PARTS + part) * 2 * cores + source],
+            far_recv.at[(chunk * COLUMN_PARTS + part) * cores + source],
             partner,
         )
 
     def far_info(target):
         return remote(
             info_rows.at[core],
-            info_rows.at[cores + outer_index * cores + core],
+            info_rows.at[cores + my_chunk * cores + core],
             info_send.at[target],
-            info_recv.at[outer_index * cores + core],
+            info_recv.at[my_chunk * cores + core],
             at_chip(far_inner, target),
+        )
+
+    def info_arrival(chunk, source):
+        return remote(
+            info_rows.at[0],
+            info_rows.at[cores + chunk * cores + source],
+            info_send.at[0],
+            info_recv.at[chunk * cores + source],
+            partner,
         )
 
     pair_info = remote(
@@ -657,10 +661,9 @@
         far_info(target).start()
     pair_tok.start()
 
-    @pl.loop(0, FAR_CHUNKS * COLUMN_PARTS)
-    def _(step):
+    for part in range(COLUMN_PARTS):
         for target in range(cores):
-            far_copy(step // COLUMN_PARTS, step % COLUMN_PARTS, target).start()
+            far_copy(part, target).start()
 
     expert_ids = lax.broadcasted_iota(jnp.int32, (chips, pooled), 0)
     near = (expert_ids // 4 == side).astype(jnp.float32)
@@ -669,7 +672,10 @@
         < lax.broadcasted_iota(jnp.int32, (pooled, pooled), 1)
     ).astype(jnp.float32).astype(jnp.bfloat16)
 
-    def rank_pool(pool, info):
+    flag_send[...] = jnp.zeros_like(flag_send)
+
+    def rank_pool(pool):
+        info = jnp.concatenate([info_rows[cores * pool + core] for core in range(cores)], axis=1)
         pool_info[pool] = info
         names = expert_ids.astype(jnp.float32)
         hot_a = (info[0:1, :] == names).astype(jnp.float32)
@@ -680,11 +686,8 @@
         count_b = jnp.sum(hot_b, axis=1, keepdims=True)
         pool_rank[pool, 0:chips, :] = hot_a * (ranks[0:chips] + 1.0)
         pool_rank[pool, chips:, :] = hot_b * (ranks[chips:] + count_a + 1.0)
-        counts = (count_a + count_b) * near
-        return jnp.max(jnp.max(counts, axis=1, keepdims=True), axis=0, keepdims=True)
-
-    def flag_of(most):
-        return jnp.broadcast_to((most > slots).astype(jnp.float32), flag_send.shape)
+        most = jnp.max((count_a + count_b) * near, axis=0, keepdims=True)[:, 0:128]
+        flag_send[...] = jnp.maximum(flag_send[...], (most > slots).astype(jnp.float32))
 
     positions = lax.broadcasted_iota(jnp.int32, (slots, pooled), 0).astype(jnp.float32) + 1.0
 
@@ -709,48 +712,27 @@
             at_chip(chip ^ mask),
         )
 
-    pair_info.wait()
-    own_most = rank_pool(0, jnp.concatenate([info_rows[0], info_rows[1]], axis=1))
-    flag_send[...] = flag_of(own_most)
-    own_tok.wait()
-    pair_tok.wait()
+    with jax.named_scope("k_own_wait"):
+        pair_info.wait()
+        rank_pool(0)
+        own_tok.wait()
+        pair_tok.wait()
 
     def pick_own(mask):
         return jnp.dot(
             chosen_rows(0, mask), tok_all[...], preferred_element_type=jnp.float32
         ).astype(jnp.bfloat16)
 
-    @pl.loop(0, 3)
+    def send_own(mask):
+        with jax.named_scope("k_own_pick"):
+            send_rows[mask] = pick_own(mask)
+            own_row_copy(mask).start()
+
+    @pl.loop(0, jnp.where(inner, 2, 3))
     def _(step):
-        mask = lax.rem(step + 1, 3) + 1
-        send_rows[mask] = pick_own(mask)
-        own_row_copy(mask).start()
+        send_own(jnp.where(step == 2, 3, 2 - step))
 
     recv_rows[0] = pick_own(0)
-
-    @pl.when(inner)
-    def _():
-        for source in range(2 * cores):
-            remote(
-                info_rows.at[0],
-                info_rows.at[cores + source],
-                info_send.at[0],
-                info_recv.at[source],
-                partner,
-            ).wait_recv()
-        left = lax.broadcasted_iota(jnp.int32, (8, rows), 1) < few
-        turned = [pltpu.roll(info_rows[cores + source], few, 1) for source in range(2 * cores)]
-        first = [
-            jnp.where(left, info_rows[cores + 2 * pair], turned[2 * pair + 1])
-            for pair in range(cores)
-        ]
-        second = [
-            jnp.where(left, turned[2 * pair], info_rows[cores + 2 * pair + 1])
-            for pair in range(cores)
-        ]
-        most_a = rank_pool(1, jnp.concatenate(first, axis=1))
-        most_b = rank_pool(2, jnp.concatenate(second, axis=1))
-        flag_send[...] = flag_of(jnp.maximum(own_most, jnp.maximum(most_a, most_b)))
 
     def flag_copy(offset):
         return remote(
@@ -760,10 +742,6 @@
             flag_rsem.at[offset],
             at_chip(lax.rem(chip + offset, chips)),
         )
-
-    @pl.loop(1, chips)
-    def _(offset):
-        flag_copy(offset).start()
 
     block = gate_mat.shape[0] // gate_scale.shape[1]
 
@@ -779,12 +757,10 @@
                     mat[at, lanes_at].astype(jnp.float32) * scale_at(strip, lane_block)
                 ).astype(jnp.bfloat16)
 
-    dequant_in_place(weight_copies[0], gate_mat, lambda row, lane: gate_scale[lane, row])
-    dequant_in_place(weight_copies[1], up_mat, lambda row, lane: up_scale[lane, row])
-    dequant_in_place(weight_copies[2], down_mat, lambda row, lane: down_scale[row, lane])
-
-    def part_cols(part):
-        return pl.ds(pl.multiple_of(part * piece, 128), piece)
+    with jax.named_scope("k_dequant"):
+        dequant_in_place(weight_copies[0], gate_mat, lambda row, lane: gate_scale[lane, row])
+        dequant_in_place(weight_copies[1], up_mat, lambda row, lane: up_scale[lane, row])
+        dequant_in_place(weight_copies[2], down_mat, lambda row, lane: down_scale[row, lane])
 
     def relay_copy(chunk, mask, part):
         target_group = 4 + 2 * chunk + mask % 2
@@ -797,10 +773,16 @@
         )
 
     def relay(chunk):
+        with jax.named_scope("k_info_wait"):
+            for source in range(cores):
+                info_arrival(chunk, source).wait_recv()
+        rank_pool(1 + chunk)
+
         @pl.loop(0, COLUMN_PARTS)
         def _(part):
-            for source in range(2 * cores):
-                far_arrival(chunk, part, source).wait_recv()
+            with jax.named_scope("k_far_wait"):
+                for source in range(cores):
+                    far_arrival(chunk, part, source).wait_recv()
 
             @pl.loop(0, 4)
             def _(step):
@@ -846,7 +828,8 @@
         )
 
     def first_half(slot_group):
-        wait_rows(slot_group)
+        with jax.named_scope("k_rows_wait"):
+            wait_rows(slot_group)
         features = recv_rows[slot_group]
         part_out[slot_group, :, 0:hidden_size] = jnp.dot(
             features, gate_mat[...], preferred_element_type=jnp.float32
@@ -873,7 +856,8 @@
         )
 
     def second_half(slot_group):
-        part_copy(slot_group).wait()
+        with jax.named_scope("k_part_wait"):
+            part_copy(slot_group).wait()
         gate = part_out[slot_group, :, 0:hidden_size].astype(jnp.float32) + part_in[
             slot_group, :, 0:hidden_size
         ].astype(jnp.float32)
@@ -895,6 +879,9 @@
             @pl.when(mask != 0)
             def _():
                 hidden_out[slot_group, :, cols] = result
+
+            @pl.when((mask != 0) & (slot_group >= 4))
+            def _():
                 back_copy(slot_group, part).start()
 
     def back_arrival(pool, mask, part):
@@ -910,7 +897,8 @@
         acc = None
         for mask in range(4):
             if mask:
-                back_arrival(pool, mask, part).wait_recv()
+                with jax.named_scope("k_back_wait"):
+                    back_arrival(pool, mask, part).wait_recv()
             in_a, in_b = slot_rows(pool, mask)
             weight = jnp.where(in_a, pool_info[pool, top_count : top_count + 1, :], 0.0)
             weight += jnp.where(in_b, pool_info[pool, top_count + 1 : top_count + 2, :], 0.0)
@@ -924,47 +912,69 @@
                 acc = product if acc is None else acc + product
         return acc
 
-    def sum_copy(chunk, part, which):
-        return remote(
-            sum_out.at[chunk, which * rows : (which + 1) * rows, part_cols(part)],
-            sum_in.at[chunk, :, part_cols(part)],
-            sum_send.at[(chunk * COLUMN_PARTS + part) * 2 + which],
-            sum_recv.at[chunk * COLUMN_PARTS + part],
-            at_chip(far_outer if which else far_inner),
-        )
-
-    def return_sums(chunk):
-        @pl.loop(0, COLUMN_PARTS)
-        def _(part):
-            sum_out[chunk, :, part_cols(part)] = combined(1 + chunk, part).astype(jnp.bfloat16)
-            for which in range(2):
-                sum_copy(chunk, part, which).start()
-
-    @pl.loop(0, 5)
+    def sum_copy(chunk, part):
+        return remote(
+            sum_out.at[chunk, :, part_cols(part)],
+            sum_in.at[:, part_cols(part)],
+            sum_send.at[chunk * COLUMN_PARTS + part],
+            sum_recv.at[part],
+            at_chip(jnp.where(chunk == 0, far_outer, far_inner)),
+        )
+
+    def return_sums(chunk, part):
+        sum_out[chunk, :, part_cols(part)] = combined(1 + chunk, part).astype(jnp.bfloat16)
+        sum_copy(chunk, part).start()
+
+    def pick_entry(turn, inner_list, outer_list):
+        value = jnp.int32(0)
+        for at, (one, two) in enumerate(zip(inner_list, outer_list)):
+            value = jnp.where(turn == at, jnp.where(inner, one, two), value)
+        return value
+
+    @pl.loop(0, len(INNER_TURNS))
     def _(turn):
-        @pl.when(inner & (turn >= 1) & (turn <= FAR_CHUNKS))
+        @pl.when(inner & ((turn == 1) | (turn == 3)))
         def _():
-            relay(turn - 1)
-
-        @pl.when(inner & (turn >= 3))
+            relay(turn // 2)
+
+        @pl.when(inner & (turn == 1))
         def _():
-            return_sums(turn - 3)
-
-        @pl.when(turn < 4)
+            send_own(3)
+
+        @pl.when(inner & (turn >= 4))
         def _():
-            position = jnp.where(
-                inner & (turn >= 1), jnp.where(turn == 3, 1, turn + 1), turn
-            )
-
-            @pl.loop(0, 2)
-            def _(which):
-                first_half(2 * position + which)
-
-            @pl.loop(0, 2)
-            def _(which):
-                second_half(2 * position + which)
-
-    flag_recv[0] = flag_send[...]
+            return_sums(turn // 2 - 2, turn % 2)
+
+        @pl.when(turn == 4)
+        def _():
+            flag_recv[0] = flag_send[...]
+
+            @pl.loop(1, chips)
+            def _(offset):
+                flag_copy(offset).start()
+
+        amount = pick_entry(turn, [len(t) for t in INNER_TURNS], [len(t) for t in OUTER_TURNS])
+        first = pick_entry(
+            turn, [(t + (0,))[0] for t in INNER_TURNS], [(t + (0,))[0] for t in OUTER_TURNS]
+        )
+        second = pick_entry(
+            turn, [(t + (0, 0))[1] for t in INNER_TURNS], [(t + (0, 0))[1] for t in OUTER_TURNS]
+        )
+
+        @pl.loop(0, amount)
+        def _(which):
+            first_half(jnp.where(which == 0, first, second))
+
+        @pl.loop(0, amount)
+        def _(which):
+            second_half(jnp.where(which == 0, first, second))
+
+        @pl.when(turn == 5)
+        def _():
+            @pl.loop(1, 4)
+            def _(mask):
+                for part in range(COLUMN_PARTS):
+                    back_copy(mask, part).start()
 
     @pl.loop(1, chips)
     def _(offset):
@@ -988,46 +998,40 @@
     def _(part):
         total[:, part_cols(part)] = combined(0, part)
 
-    def out_rows(owner, chunk):
-        return pl.ds(pl.multiple_of(owner * rows + chunk * few, few), few)
-
     def out_cols(part):
         return pl.ds(pl.multiple_of(core * half + part * piece, 128), piece)
 
-    def own_out(chunk, part):
+    def own_out(part):
         return pltpu.make_async_copy(
-            mixed.at[out_rows(core, chunk), part_cols(part)],
-            out.at[chunk * few : (chunk + 1) * few, out_cols(part)],
-            out_sem.at[chunk * COLUMN_PARTS + part],
-        )
-
-    def pair_out(chunk, part):
-        return remote(
-            mixed.at[out_rows(other, chunk), part_cols(part)],
-            out.at[chunk * few : (chunk + 1) * few, out_cols(part)],
-            out_send.at[chunk * COLUMN_PARTS + part],
-            out_recv.at[chunk * COLUMN_PARTS + part],
+            mixed.at[my_rows, part_cols(part)],
+            out.at[:, out_cols(part)],
+            out_sem.at[part],
+        )
+
+    def pair_out(part):
+        return remote(
+            mixed.at[your_rows, part_cols(part)],
+            out.at[:, out_cols(part)],
+            out_send.at[part],
+            out_recv.at[part],
             partner,
         )
 
-    for chunk in range(FAR_CHUNKS):
-        for part in range(COLUMN_PARTS):
-            cols = slice(part * piece, (part + 1) * piece)
+    for part in range(COLUMN_PARTS):
+        cols = slice(part * piece, (part + 1) * piece)
+        with jax.named_scope("k_sum_wait"):
             remote(
-                sum_out.at[0, 0:rows, cols],
-                sum_in.at[chunk, :, cols],
+                sum_out.at[0, :, cols],
+                sum_in.at[:, cols],
                 sum_send.at[0],
-                sum_recv.at[chunk * COLUMN_PARTS + part],
+                sum_recv.at[part],
                 partner,
             ).wait_recv()
-            for owner in range(cores):
-                at = slice(owner * rows + chunk * few, owner * rows + (chunk + 1) * few)
-                mixed[at, cols] = (
-                    total[at, cols]
-                    + sum_in[chunk, owner * few : (owner + 1) * few, cols].astype(jnp.float32)
-                ).astype(jnp.bfloat16)
-            pair_out(chunk, part).start()
-            own_out(chunk, part).start()
+        mixed[:, cols] = (total[:, cols] + sum_in[:, cols].astype(jnp.float32)).astype(
+            jnp.bfloat16
+        )
+        pair_out(part).start()
+        own_out(part).start()
 
     for copy in far_copies:
         copy.wait()
@@ -1036,10 +1040,9 @@
     for target in range(cores):
         far_info(target).wait_send()
 
-    @pl.loop(0, FAR_CHUNKS * COLUMN_PARTS)
-    def _(step):
+    for part in range(COLUMN_PARTS):
         for target in range(cores):
-            far_copy(step // COLUMN_PARTS, step % COLUMN_PARTS, target).wait_send()
+            far_copy(part, target).wait_send()
 
     @pl.loop(1, 4)
     def _(mask):
@@ -1060,17 +1063,15 @@
         def _(step):
             chunk = step // COLUMN_PARTS
             part = step % COLUMN_PARTS
-            for which in range(2):
-                sum_copy(chunk, part, which).wait_send()
+            sum_copy(chunk, part).wait_send()
 
             @pl.loop(1, 4)
             def _(mask):
                 relay_copy(chunk, mask, part).wait_send()
 
-    for chunk in range(FAR_CHUNKS):
-        for part in range(COLUMN_PARTS):
-            own_out(chunk, part).wait()
-            pair_out(chunk, part).wait()
+    for part in range(COLUMN_PARTS):
+        own_out(part).wait()
+        pair_out(part).wait()
 
 
 def two_level_call(slots, tok_rows, half, hidden_size, groups, weight_shapes):
@@ -1107,7 +1108,7 @@
             pltpu.VMEM((8, slots, half), bf16),
             pltpu.VMEM((12, slots, half), bf16),
             pltpu.VMEM((FAR_CHUNKS, pooled, half), bf16),
-            pltpu.VMEM((FAR_CHUNKS, tok_rows, half), bf16),
+            pltpu.VMEM((pooled, half), bf16),
             pltpu.VMEM((pooled, half), f32),
             pltpu.VMEM((pooled, half), bf16),
             pltpu.VMEM((8, 128), f32),
@@ -1119,19 +1120,19 @@
             dma((2,)),
             dma((cores,)),
             dma((2 * cores,)),
+            dma((COLUMN_PARTS * cores,)),
             dma((pieces * cores,)),
-            dma((pieces * 2 * cores,)),
             dma((12 * COLUMN_PARTS,)),
             dma((8 * COLUMN_PARTS,)),
             dma((8,)),
             dma((8,)),
             dma((8 * COLUMN_PARTS,)),
             dma((12 * COLUMN_PARTS,)),
-            dma((pieces * 2,)),
             dma((pieces,)),
-            dma((pieces,)),
-            dma((pieces,)),
-            dma((pieces,)),
+            dma((COLUMN_PARTS,)),
+            dma((COLUMN_PARTS,)),
+            dma((COLUMN_PARTS,)),
+            dma((COLUMN_PARTS,)),
             dma((chips,)),
             dma((chips,)),
             dma((groups,)),

time: 145 us -> 112 us (0.77); the launches traced: 145 us -> 110 us
  Pallas kernels: 142 us -> 107 us
    pallas_call x1, Pallas kernels: 142 us -> 107 us  [per_device(): out, flag = call(*args)]
where the time goes in v2:
time: 112 us; the launch traced here: 110 us
  Pallas kernels  107 us (96%)
  local copies, waits for them, and re-layouts  2.19 us (2%)
    pallas_call x1, Pallas kernels, per_device(): out, flag = call(*args)  107 us

profile of v2, /device:TPU:0, one launch (start us, length us, event | category | flops | bytes accessed | tf_op | source)
XLA Modules:
  0.0 110.0 jit_solution(3587758565675760962)
XLA Ops:
  0.0 0.0 copy-start.1
  0.0 0.0 copy-start.3
  0.0 0.0 copy-start.4
  0.0 0.0 copy-start.5
  0.0 0.0 copy-start.6
  0.0 0.0 copy-start.7
  0.0 0.0 copy-start.8
  0.0 0.0 copy-start.9
  0.0 106.9 %shard_map.111 = (bf16[128,3584]{1,0:T(8,128)(2,1)}, s32[1]{0:T(128)}) custom-call(bf16[128,3584]{1,0:T(8,128)(2,1)} %tokens.1, s32[2,128]{1,0:T(2,128)} %bitcast.80, s32[2,128]{1,0:T(2,128)} %bitcast.81, f32[2,128]{1,0:T(2,128)} %bitcast.82, s32[8]{0:T(128)} %hot.1, bf16[1,1792,1024]{2,1,0:T(8,128)(2,1)} %w_gate.1, bf16[1,1792,1024]{2,1,0:T(8,128)(2,1)} %w_up.1, ...), custom_call_target="tpu_custom_call" | custom-call | tf_op jit(solution)/shard_map/pallas_call | solution.py:1237
  107.5 0.0 copy-done.1
  107.6 0.0 copy-done.3
  107.6 0.0 copy-done.4
  107.6 0.0 copy-done.5
  107.6 0.0 copy-done.6
  107.6 0.0 copy-done.7
  107.6 0.0 copy-done.8
  107.6 0.0 copy-done.9
  107.6 0.2 conditional.1
  107.9 2.2 %copy.38 = bf16[128,3584]{1,0:T(8,128)(2,1)} copy(bf16[128,3584]{1,0:T(8,128)(2,1)} %get-tuple-element.46) | data formatting | bytes 1835008
Async XLA Ops:
  0.0 107.5 %copy-start.1 = (bf16[128,3584]{1,0:T(8,128)(2,1)S(1)}, bf16[128,3584]{1,0:T(8,128)(2,1)}, u32[]{:S(2)}) copy-start(bf16[128,3584]{1,0:T(8,128)(2,1)} %tokens.1) | copy-start | bytes 2752516
  0.0 107.6 %copy-start.3 = (f32[1,14,8]{1,2,0:T(8,128)S(1)}, f32[1,14,8]{1,2,0:T(8,128)}, u32[]{:S(2)}) copy-start(f32[1,14,8]{1,2,0:T(8,128)} %param.21) | copy-start | bytes 1348
  0.0 107.6 %copy-start.4 = (f32[1,14,8]{1,2,0:T(8,128)S(1)}, f32[1,14,8]{1,2,0:T(8,128)}, u32[]{:S(2)}) copy-start(f32[1,14,8]{1,2,0:T(8,128)} %param.22) | copy-start | bytes 1348
  0.0 107.6 %copy-start.5 = (f32[1,8,14]{2,1,0:T(8,128)S(1)}, f32[1,8,14]{2,1,0:T(8,128)}, u32[]{:S(2)}) copy-start(f32[1,8,14]{2,1,0:T(8,128)} %param.23) | copy-start | bytes 1348
  0.0 107.6 %copy-start.6 = (s32[128,2]{0,1:T(2,128)S(1)}, s32[128,2]{0,1:T(2,128)}, u32[]{:S(2)}) copy-start(s32[128,2]{0,1:T(2,128)} %param.14) | copy-start | bytes 3076
  0.0 107.6 %copy-start.7 = (s32[128,2]{0,1:T(2,128)S(1)}, s32[128,2]{0,1:T(2,128)}, u32[]{:S(2)}) copy-start(s32[128,2]{0,1:T(2,128)} %param.15) | copy-start | bytes 3076
  0.0 107.6 %copy-start.8 = (f32[128,2]{0,1:T(2,128)S(1)}, f32[128,2]{0,1:T(2,128)}, u32[]{:S(2)}) copy-start(f32[128,2]{0,1:T(2,128)} %param.16) | copy-start | bytes 3076
  0.0 107.6 %copy-start.9 = (s32[8]{0:T(128)S(1)}, s32[8]{0:T(128)}, u32[]{:S(2)}) copy-start(s32[8]{0:T(128)} %hot.1) | copy-start | bytes 100
